TPU v7x, 32 devices: a whole 2x2x4 slice. The times are simulated.
32 devices in a mesh: row: 2 (over core), sa: 16 (over z, y, x).
Axes of the slice: x: 2, y: 2, z: 4, core: 2. Of those that a mesh axis runs over, the one named last changes fastest.
Arguments:
- rep_w1: float32 [4, 2, 64, 4096], P('row', None, None, 'sa'), may hold values from -6 to 6
- rep_w3: float32 [4, 2, 64, 4096], P('row', None, None, 'sa'), may hold values from -6 to 6
- rep_w2: float32 [4, 2, 64, 4096], P('row', None, None, 'sa'), may hold values from -6 to 6
- rep_gate: float32 [4, 2, 4096], P('row', None, 'sa'), may hold values from -6 to 6
Outputs:
- serve_w1: bfloat16 [2, 64, 4096], P('row', 'sa')
- serve_w3: bfloat16 [2, 64, 4096], P('row', 'sa')
- serve_w2: bfloat16 [2, 64, 4096], P('row', 'sa')
- serve_gate: bfloat16 [2, 4096], replicated
- soup_norms: float32 [2, 4], P('row')
- replica_norms: float32 [4, 2, 4], P('row')
All inputs are finite; a program needn't handle non-finite values.
Results may differ from a plain program's by a relative error of at most 0.001.
Values may be sent and summed in bfloat16 or wider, within the bound.
A program may use at most 64 MiB of HBM per device.

v0:
```python
import jax
import jax.numpy as jnp
from jax import lax
from jax.sharding import PartitionSpec as P


def own_rows_2(product, width, axis):
    everything = product(jnp.int32(0), lax.axis_size(axis) * width)
    own = lax.psum_scatter(everything, axis, scatter_dimension=0, tiled=True)
    return own


def square_sums(values, dims_summed):
    return jnp.sum(values * values, axis=dims_summed)


def local(rep_w1, rep_w3, rep_w2, rep_gate):
    rows_total = lax.axis_size("row")
    replicas = rep_w1.shape[0] * rows_total
    experts_all = rep_w1.shape[1]
    expert_rows = experts_all // rows_total
    hidden_all = rep_w1.shape[2]
    model_width = rep_w1.shape[3] * lax.axis_size("sa")
    weights = (rep_w1, rep_w3, rep_w2)
    replica_parts = jnp.stack(
        [square_sums(weight, (2, 3)) for weight in weights] + [square_sums(rep_gate, 2)], axis=2
    )

    def expert_terms(offset, length):
        pieces = [
            jnp.sum(lax.dynamic_slice_in_dim(weight, offset, length, 1), axis=0)
            for weight in weights
        ]
        return jnp.stack(pieces, axis=1)

    summed = own_rows_2(expert_terms, expert_rows, "row")
    served = (summed / replicas).astype(jnp.bfloat16)
    arranged = lax.all_to_all(served, "sa", split_axis=2, concat_axis=3, tiled=True)
    served_list = [arranged[:, column] for column in range(3)]
    gate_local = jnp.sum(rep_gate, axis=0)
    gate_total = lax.psum(gate_local, "row")
    gate_shard = (gate_total / replicas).astype(jnp.bfloat16)
    serve_gate = lax.all_gather(gate_shard, "sa", axis=1, tiled=True)
    own_rows = lax.dynamic_slice_in_dim(
        gate_shard, lax.axis_index("row") * expert_rows, expert_rows, 0
    )
    soup_parts = jnp.stack(
        [square_sums(served.astype(jnp.float32), (1, 2)) for served in served_list]
        + [square_sums(own_rows.astype(jnp.float32), 1)],
        axis=1,
    )
    replica_total, soup_total = lax.psum((replica_parts, soup_parts), "sa")
    counts = jnp.array([hidden_all * model_width] * 3 + [model_width], jnp.float32)
    replica_norms = jnp.sqrt(replica_total / counts)
    soup_norms = jnp.sqrt(soup_total / counts)
    return (served_list[0], served_list[1], served_list[2], serve_gate, soup_norms, replica_norms)


def solution(mesh):
    placed = (
        P("row", None, None, "sa"),
        P("row", None, None, "sa"),
        P("row", None, None, "sa"),
        P("row", None, "sa"),
    )
    return jax.shard_map(
        local,
        mesh=mesh,
        in_specs=placed,
        out_specs=(
            P("row", "sa", None),
            P("row", "sa", None),
            P("row", "sa", None),
            P(),
            P("row", None),
            P("row", None, None),
        ),
        check_vma=False,
    )
```

profile of v0, /device:TPU:0, one launch (start us, length us, event | category | flops | bytes accessed | tf_op | source)
XLA Modules:
  0.0 122.1 jit_solution(15603964799628544858)
XLA Ops:
  7.2 0.0 copy-start
  7.2 0.0 reduce-scatter.2.cloned.1.call-start
  7.2 1.1 multiply_reduce_fusion.2
  8.3 0.0 copy-done
  8.3 1.1 multiply_reduce_fusion
  9.5 0.8 copy.15
  10.3 0.0 copy-start.1
  10.3 0.0 reduce-scatter.2.cloned.1.call-update
  10.3 0.7 copy-done.1
  11.0 0.1 multiply_reduce_fusion.6
  11.0 2.6 %psum.21 = f32[2,256]{1,0:T(2,128)S(1)} all-reduce(f32[2,256]{1,0:T(2,128)S(1)} %get-tuple-element.37), channel_id=1, replica_groups=mesh['row'=2,'sa'=16] {'row'}, use_global_device_ids=true, to_apply=%region_5.0 | all-reduce | flops 512 | bytes 4096 | tf_op jit(solution)/shard_map/psum | solution.py:41
  13.7 7.4 %reduce-scatter.2.cloned.1.call-done = f32[1,3,64,256]{3,2,1,0:T(8,128)} async-done(((f32[2,3,64,256]{3,2,1,0:T(8,128)}), f32[1,3,64,256]{3,2,1,0:T(8,128)}) %reduce-scatter.2.cloned.1.call-update) | async-done | bytes 196624 | tf_op jit(solution)/shard_map/reduce_scatter | solution.py:9
  21.0 0.9 multiply_convert_fusion
  21.9 0.7 copy.16
  22.7 6.7 %all-to-all-start = ((bf16[1,3,64,256]{3,1,0,2:T(4,128)(2,1)}), bf16[1,3,64,256]{3,1,0,2:T(4,128)(2,1)S(1)}, u32[]{:S(2)}, u32[]{:S(2)}) async-start(bf16[1,3,64,256]{3,1,0,2:T(4,128)(2,1)} %copy.16), calls=%async_computation.1 | async-start | bytes 262144 | tf_op jit(solution)/shard_map/all_to_all | solution.py:38
  29.4 0.6 multiply_reduce_fusion.7
  30.0 41.0 %all_gather.3 = bf16[2,4096]{1,0:T(2,128)(2,1)S(1)} all-gather(bf16[2,256]{1,0:T(2,128)(2,1)S(1)} %multiply_convert_fusion.1), channel_id=1, replica_groups=mesh['row'=2,'sa'=16] {'sa'}, dimensions={1}, use_global_device_ids=true | all-gather | bytes 17408 | tf_op jit(solution)/shard_map/all_gather | solution.py:43
  71.0 0.0 all-to-all-done
  71.1 1.3 %multiply_reduce_fusion.3 = (f32[]{:T(128)}, bf16[1,4,4096]{2,1,0:T(4,128)(2,1)}, f32[]{:T(128)}, bf16[1,4,4096]{2,1,0:T(4,128)(2,1)}, f32[]{:T(128)}, /*index=5*/bf16[1,4,4096]{2,1,0:T(4,128)(2,1)}) fusion(bf16[1,3,4,4096]{3,2,1,0:T(4,128)(2,1)S(1)} %bitcast.28), kind=kLoop, calls=%fused_computation.5 | loop fusion | flops 147453 | bytes 196620 | tf_op jit(solution)/shard_map/reduce_sum | solution.py:14
  72.4 2.6 %pad_maximum_fusion.2 = f32[1,4]{1,0:T(1,128)S(1)} fusion(f32[1,1]{1,0:T(1,128)} %bitcast.13, f32[1,1]{1,0:T(1,128)} %bitcast.12, f32[1,1]{1,0:T(1,128)} %bitcast.11, f32[1,1]{1,0:T(1,128)} %bitcast.10), kind=kLoop, calls=%fused_computation.16 | loop fusion | flops 12 | bytes 32 | tf_op jit(solution)/shard_map/stack | solution.py:47
  75.0 37.0 %all-reduce = (f32[1,4]{1,0:T(1,128)S(1)}, f32[2,2,4]{1,0,2:T(2,128)S(1)}) all-reduce(f32[1,4]{1,0:T(1,128)S(1)} %pad_maximum_fusion.2, f32[2,2,4]{1,0,2:T(2,128)S(1)} %pad_maximum_fusion.1), channel_id=1, replica_groups=mesh['row'=2,'sa'=16] {'sa'}, use_global_device_ids=true, to_apply=%region_10.0 | all-reduce | flops 20 | bytes 160 | tf_op jit(solution)/shard_map/psum | solution.py:52
  112.0 0.0 copy-start.2
  112.0 0.6 copy-done.2
  112.7 0.1 multiply_sqrt_fusion
  112.8 0.7 copy.18
  113.4 0.0 copy-start.3
  113.4 0.7 copy-done.3
  114.1 0.5 multiply_sqrt_fusion.1
  114.6 0.6 copy.21
  (4 shorter events, 0.1 us)
Async XLA Ops:
  7.2 1.2 copy-start
  7.2 13.8 %reduce-scatter.2.cloned.1.call-start = ((), (), s32[]{:S(2)}) async-start(), calls=%async_computation.2 | async-start | bytes 589824 | tf_op jit(solution)/shard_map/reduce_scatter | solution.py:9
  10.3 0.7 copy-start.1
  22.7 48.4 %all-to-all-start = ((bf16[1,3,64,256]{3,1,0,2:T(4,128)(2,1)}), bf16[1,3,64,256]{3,1,0,2:T(4,128)(2,1)S(1)}, u32[]{:S(2)}, u32[]{:S(2)}) async-start(bf16[1,3,64,256]{3,1,0,2:T(4,128)(2,1)} %copy.16), calls=%async_computation.1 | async-start | bytes 262144 | tf_op jit(solution)/shard_map/all_to_all | solution.py:38
  112.0 0.7 copy-start.2
  113.4 0.7 copy-start.3
Sparse Core Ops, SparseCore 0:
  10.4 10.5 reduce-scatter.1
where the time goes:
time: 122 us
  blocking collectives  80.7 us (66%)
  between operations  14.1 us (12%)
  other arithmetic  8.38 us (7%)
  waiting for transfers between devices  7.37 us (6%)
  starting transfers between devices  6.75 us (6%)
  local copies, waits for them, and re-layouts  4.79 us (4%)
    all_gather x1, blocking collectives, local(): serve_gate = lax.all_gather(gate_shard, 'sa', axis=1, tiled=True)  41 us
    psum x1, blocking collectives, local(): replica_total, soup_total = lax.psum((replica_parts, soup_parts), 'sa')  37 us
    reduce_scatter x1, waiting for transfers between devices, own_rows_2(): own = lax.psum_scatter(everything, axis, scatter_dimension=0, tiled=True)  7.35 us
    all_to_all x1, starting transfers between devices, local(): lax.all_to_all(served, 'sa', split_axis=2, concat_axis=3, tiled=True)  6.72 us
    reduce_sum x5, other arithmetic, square_sums(): return jnp.sum(values * values, axis=dims_summed)  4.24 us
    unnamed x10, local copies, waits for them, and re-layouts  3.25 us
    psum x1, blocking collectives, local(): gate_total = lax.psum(gate_local, 'row')  2.6 us
    another operation x1, other arithmetic, local(): jnp.stack([square_sums(served.astype(jnp.float32), (1, 2)) for served in...  2.57 us
  transfers between devices with their start and end apart: 2, of which 1 were waited for; matrix products, arithmetic and copies ran while one was open for 1% of the time, Pallas kernels for 0%

commit v1 on v0

--- a/solution.py
+++ b/solution.py
@@ -40,7 +40,8 @@
     gate_local = jnp.sum(rep_gate, axis=0)
     gate_total = lax.psum(gate_local, "row")
     gate_shard = (gate_total / replicas).astype(jnp.bfloat16)
-    serve_gate = lax.all_gather(gate_shard, "sa", axis=1, tiled=True)
+    parts = lax.all_gather(gate_shard, "sa")
+    serve_gate = jnp.concatenate(parts, axis=1)
     own_rows = lax.dynamic_slice_in_dim(
         gate_shard, lax.axis_index("row") * expert_rows, expert_rows, 0
     )

time: 122 us -> 122 us (level)
  no operation moved by 1% of the time
where the time goes in v1:
time: 122 us
  blocking collectives  80.7 us (66%)
  between operations  14.1 us (12%)
  other arithmetic  8.39 us (7%)
  waiting for transfers between devices  7.37 us (6%)
  starting transfers between devices  6.75 us (6%)
  local copies, waits for them, and re-layouts  4.79 us (4%)
    all_gather x1, blocking collectives, local(): parts = lax.all_gather(gate_shard, 'sa')  41 us
    psum x1, blocking collectives, local(): replica_total, soup_total = lax.psum((replica_parts, soup_parts), 'sa')  37 us
    reduce_scatter x1, waiting for transfers between devices, own_rows_2(): own = lax.psum_scatter(everything, axis, scatter_dimension=0, tiled=True)  7.35 us
    all_to_all x1, starting transfers between devices, local(): lax.all_to_all(served, 'sa', split_axis=2, concat_axis=3, tiled=True)  6.72 us
    reduce_sum x5, other arithmetic, square_sums(): return jnp.sum(values * values, axis=dims_summed)  4.24 us
    unnamed x10, local copies, waits for them, and re-layouts  3.25 us
    psum x1, blocking collectives, local(): gate_total = lax.psum(gate_local, 'row')  2.6 us
    another operation x1, other arithmetic, local(): jnp.stack([square_sums(served.astype(jnp.float32), (1, 2)) for served in...  2.57 us
  transfers between devices with their start and end apart: 2, of which 1 were waited for; matrix products, arithmetic and copies ran while one was open for 1% of the time, Pallas kernels for 0%

profile of v1, /device:TPU:0, one launch (start us, length us, event | category | flops | bytes accessed | tf_op | source)
XLA Modules:
  0.0 122.1 jit_solution(10588655764540912956)
XLA Ops:
  7.2 0.0 copy-start
  7.2 0.0 reduce-scatter.2.cloned.1.call-start
  7.2 1.1 multiply_reduce_fusion.2
  8.3 0.0 copy-done
  8.3 1.1 multiply_reduce_fusion
  9.5 0.8 copy.15
  10.3 0.0 copy-start.1
  10.3 0.0 reduce-scatter.2.cloned.1.call-update
  10.3 0.7 copy-done.1
  11.0 0.1 multiply_reduce_fusion.6
  11.0 2.6 %psum.21 = f32[2,256]{1,0:T(2,128)S(1)} all-reduce(f32[2,256]{1,0:T(2,128)S(1)} %get-tuple-element.37), channel_id=1, replica_groups=mesh['row'=2,'sa'=16] {'row'}, use_global_device_ids=true, to_apply=%region_5.0 | all-reduce | flops 512 | bytes 4096 | tf_op jit(solution)/shard_map/psum | solution.py:41
  13.7 7.3 %reduce-scatter.2.cloned.1.call-done = f32[1,3,64,256]{3,2,1,0:T(8,128)} async-done(((f32[2,3,64,256]{3,2,1,0:T(8,128)}), f32[1,3,64,256]{3,2,1,0:T(8,128)}) %reduce-scatter.2.cloned.1.call-update) | async-done | bytes 196624 | tf_op jit(solution)/shard_map/reduce_scatter | solution.py:9
  21.0 0.9 multiply_convert_fusion
  21.9 0.7 copy.16
  22.7 6.7 %all-to-all-start = ((bf16[1,3,64,256]{3,1,0,2:T(4,128)(2,1)}), bf16[1,3,64,256]{3,1,0,2:T(4,128)(2,1)S(1)}, u32[]{:S(2)}, u32[]{:S(2)}) async-start(bf16[1,3,64,256]{3,1,0,2:T(4,128)(2,1)} %copy.16), calls=%async_computation.1 | async-start | bytes 262144 | tf_op jit(solution)/shard_map/all_to_all | solution.py:38
  29.4 0.6 multiply_reduce_fusion.7
  30.0 41.0 %all-gather.1 = bf16[16,2,256]{2,1,0:T(2,128)(2,1)S(1)} all-gather(bf16[1,2,256]{2,1,0:T(2,128)(2,1)S(1)} %fusion), channel_id=2, replica_groups=mesh['row'=2,'sa'=16] {'sa'}, dimensions={0}, use_global_device_ids=true | all-gather | bytes 17408 | tf_op jit(solution)/shard_map/all_gather | solution.py:43
  71.0 0.0 all-to-all-done
  71.1 1.3 %multiply_reduce_fusion.3 = (f32[]{:T(128)}, bf16[1,4,4096]{2,1,0:T(4,128)(2,1)}, f32[]{:T(128)}, bf16[1,4,4096]{2,1,0:T(4,128)(2,1)}, f32[]{:T(128)}, /*index=5*/bf16[1,4,4096]{2,1,0:T(4,128)(2,1)}) fusion(bf16[1,3,4,4096]{3,2,1,0:T(4,128)(2,1)S(1)} %bitcast.33), kind=kLoop, calls=%fused_computation.5 | loop fusion | flops 147453 | bytes 196620 | tf_op jit(solution)/shard_map/reduce_sum | solution.py:14
  72.4 2.6 %pad_maximum_fusion.2 = f32[1,4]{1,0:T(1,128)S(1)} fusion(f32[1,1]{1,0:T(1,128)} %bitcast.16, f32[1,1]{1,0:T(1,128)} %bitcast.15, f32[1,1]{1,0:T(1,128)} %bitcast.14, f32[1,1]{1,0:T(1,128)} %bitcast.13), kind=kLoop, calls=%fused_computation.16 | loop fusion | flops 12 | bytes 32 | tf_op jit(solution)/shard_map/stack | solution.py:48
  75.0 37.0 %all-reduce = (f32[1,4]{1,0:T(1,128)S(1)}, f32[2,2,4]{1,0,2:T(2,128)S(1)}) all-reduce(f32[1,4]{1,0:T(1,128)S(1)} %pad_maximum_fusion.2, f32[2,2,4]{1,0,2:T(2,128)S(1)} %pad_maximum_fusion.1), channel_id=1, replica_groups=mesh['row'=2,'sa'=16] {'sa'}, use_global_device_ids=true, to_apply=%region_10.0 | all-reduce | flops 20 | bytes 160 | tf_op jit(solution)/shard_map/psum | solution.py:53
  112.0 0.0 copy-start.2
  112.0 0.6 copy-done.2
  112.7 0.1 multiply_sqrt_fusion
  112.8 0.7 copy.18
  113.4 0.0 copy-start.3
  113.4 0.7 copy-done.3
  114.1 0.5 multiply_sqrt_fusion.1
  114.6 0.6 copy.21
  (5 shorter events, 0.1 us)
Async XLA Ops:
  7.2 1.2 copy-start
  7.2 13.8 %reduce-scatter.2.cloned.1.call-start = ((), (), s32[]{:S(2)}) async-start(), calls=%async_computation.2 | async-start | bytes 589824 | tf_op jit(solution)/shard_map/reduce_scatter | solution.py:9
  10.3 0.7 copy-start.1
  22.7 48.4 %all-to-all-start = ((bf16[1,3,64,256]{3,1,0,2:T(4,128)(2,1)}), bf16[1,3,64,256]{3,1,0,2:T(4,128)(2,1)S(1)}, u32[]{:S(2)}, u32[]{:S(2)}) async-start(bf16[1,3,64,256]{3,1,0,2:T(4,128)(2,1)} %copy.16), calls=%async_computation.1 | async-start | bytes 262144 | tf_op jit(solution)/shard_map/all_to_all | solution.py:38
  112.0 0.7 copy-start.2
  113.4 0.7 copy-start.3
Sparse Core Ops, SparseCore 0:
  10.4 10.5 reduce-scatter.1
